TPU v7x, 32 devices: a whole 2x2x4 slice. The times are simulated.
32 devices in a mesh: groups: 2 (over x), ty: 8 (over z, y), tx: 2 (over core).
Axes of the slice: x: 2, y: 2, z: 4, core: 2. Of those that a mesh axis runs over, the one named last changes fastest.
Arguments:
- fields: bfloat16 [6, 2048, 1024], P(None, ('groups', 'ty'), 'tx'), parts along dimension 1, may hold values from -8 to 8
- weights: bfloat16 [2048, 1024], P(('groups', 'ty'), 'tx'), parts along dimension 0, may hold values from 0.049804688 to 0.94921875
- source_tile: int32 [16, 8, 2], P(('groups', 'ty'), 'tx'), parts along dimension 0, may hold values from 0 to 15, as said below
- source_block: int32 [16, 8, 2], P(('groups', 'ty'), 'tx'), parts along dimension 0, may hold values from 0 to 3
- coupling: bfloat16 [6, 6], replicated, may hold values from -2.5 to 2.5
- driver: float32 [6, 128, 128], replicated, may hold values from -48 to 48
- relaxation: float32 [6, 128, 128], replicated, may hold values from 0.05 to 0.6
Outputs:
- nudged: float32 [6, 2048, 1024], P(None, ('groups', 'ty'), 'tx'), parts along dimension 1
There are 2 independent parts, one for each index of `groups`. A program takes and returns all parts, laid end to end along the dimension named above; an argument that names none is the same for every part. Nothing has to cross between parts.
Inputs may be any that keep to these rules, and one draw needn't show every extreme that they name: `source_tile`: the two sources of a block lie in the same block row, the second one block column east of the first (wrapping around the domain). Among the 8 requests of one tile, no tile row of owners is named more than 4 times, and in every tile some owner tile is named exactly 4 times.
All inputs are finite; a program needn't handle non-finite values.
Results may differ from a plain program's by a relative error of at most 0.0003.
Values may be sent and summed in bfloat16 or wider, within the bound.
A program may use at most 128 MiB of HBM per device.

v0:
```python
import functools
import math

import jax
import jax.numpy as jnp
import numpy as np
from jax import lax
from jax.experimental import pallas as pl
from jax.experimental.pallas import tpu as pltpu
from jax.sharding import PartitionSpec as P

BS = 128
KMAX = 64
GROUP = 2
MESH = pl.DeviceIdType.MESH
HI = lax.Precision.HIGHEST


def wave_table(period):
    position = np.arange(period, dtype=np.int64)[:, None]
    mode = np.arange(KMAX, dtype=np.int64)[None, :]
    norming = np.where(mode == 0, math.sqrt(1.0 / period), math.sqrt(2.0 / period))
    cos_part = np.cos(2.0 * math.pi * (position * mode % period) / period) * norming
    sin_part = np.sin(2.0 * math.pi * (position * (mode + 1) % period) / period) * math.sqrt(2.0 / period)
    return np.concatenate([cos_part, sin_part], axis=1).astype(np.float32)


def two_lines(mesh):
    devices = np.asarray(mesh.devices)
    axis = list(mesh.axis_names).index("ty")
    line = np.moveaxis(devices, axis, 0).reshape(devices.shape[axis], -1)[:, 0]
    coords = [getattr(d, "coords", None) for d in line]
    if any(c is None for c in coords) or len(line) % 2:
        return False
    varying = [k for k in range(len(coords[0])) if len({c[k] for c in coords}) > 1]
    return len(varying) > 1


def kernel(
    n_ty, n_tx, snake,
    fields, weights_hbm, picks, coupling, driver_hbm, relaxation_hbm, row_tab, row_tab_t, col_tab,
    out, *scratch,
):
    n_fields, rows, cols = fields.shape
    gathered = scratch[:n_fields]
    n_groups = n_fields // GROUP
    (modes, swapped, chip_sums, rs_bufs, sums, ag_bufs) = (
        scratch[n_fields + k * n_groups : n_fields + (k + 1) * n_groups] for k in range(6))
    (row_b, row_bt, col_b, weights, driver, relaxation, tab_sem, own_sem, ring_send, ring_recv, mate_send, mate_recv,
     rs_send, rs_recv, ag_send, ag_recv, swap_send, swap_recv, back_send, back_recv) = scratch[n_fields + 6 * n_groups :]
    per_tile = cols // BS
    ty = lax.axis_index("ty")
    tx = lax.axis_index("tx")
    mate = 1 - tx
    depth = n_ty // 2

    def ring_to_ty(pos):
        pos = (pos + n_ty) % n_ty
        if not snake:
            return pos
        return jnp.where(pos < n_ty // 2, 2 * pos, 2 * (n_ty - 1 - pos) + 1)

    ring = jnp.where(ty % 2 == 0, ty // 2, n_ty - 1 - ty // 2) if snake else ty
    toward = (ring_to_ty(ring + 1), ring_to_ty(ring - 1))

    tabs = [
        pltpu.make_async_copy(row_tab.at[pl.ds(ty * rows, rows), :], row_b, tab_sem.at[0]),
        pltpu.make_async_copy(row_tab_t.at[:, pl.ds(pl.multiple_of(ty * rows, 128), rows)], row_bt, tab_sem.at[1]),
        pltpu.make_async_copy(col_tab.at[pl.ds(tx * cols, cols), :], col_b, tab_sem.at[2]),
        pltpu.make_async_copy(weights_hbm, weights, tab_sem.at[3]),
        pltpu.make_async_copy(driver_hbm, driver, tab_sem.at[4]),
        pltpu.make_async_copy(relaxation_hbm, relaxation, tab_sem.at[5]),
    ]

    def tile_of(f, col, row, part=None):
        first, count = (col * n_ty + row) * per_tile, per_tile
        if part is not None:
            count = per_tile // 2
            first = first + part * count
        return gathered[f].at[pl.ds(first, count)]

    def column_of(f, col):
        return gathered[f].at[pl.ds(col * n_ty * per_tile, n_ty * per_tile)]

    barrier = pltpu.get_barrier_semaphore()
    pl.semaphore_signal(barrier, inc=1, device_id={"tx": mate}, device_id_type=MESH)
    for k in range(1, n_ty):
        pl.semaphore_signal(barrier, inc=1, device_id={"ty": (ty + k) % n_ty}, device_id_type=MESH)
    here = (tx * n_ty + ty) * per_tile

    own = [
        pltpu.make_async_copy(fields.at[f, :, pl.ds(b * BS, BS)], gathered[f].at[here + b], own_sem.at[f, b])
        for f in range(n_fields)
        for b in range(per_tile)
    ]
    for copy in own + tabs:
        copy.start()
    pl.semaphore_wait(barrier, n_ty)
    for copy in own:
        copy.wait()

    def to_mate(f, ref):
        return pltpu.make_async_remote_copy(
            src_ref=ref, dst_ref=ref, send_sem=mate_send.at[f], recv_sem=mate_recv.at[f],
            device_id={"tx": mate}, device_id_type=MESH)

    def sign(way):
        return 1 if way == 0 else -1

    def travels(way, h, d):
        return d < depth - 1 or (d == depth - 1 and h == way)

    def ring_copy(f, way, h, d):
        ref = tile_of(f, tx, ring_to_ty(ring - sign(way) * d), h)
        return pltpu.make_async_remote_copy(
            src_ref=ref, dst_ref=ref,
            send_sem=ring_send.at[f], recv_sem=ring_recv.at[f, way, h, d],
            device_id={"ty": toward[way]}, device_id_type=MESH)

    def arrived(f, way, h, d):
        ref = tile_of(f, tx, ring_to_ty(ring - sign(way) * (d + 1)), h)
        pltpu.make_async_remote_copy(
            src_ref=ref, dst_ref=ref, send_sem=ring_send.at[f], recv_sem=ring_recv.at[f, way, h, d],
            device_id={"ty": toward[way]}, device_id_type=MESH).wait_recv()
        return ref

    def stage(g, d):
        for f in range(g * GROUP, (g + 1) * GROUP):
            for h in range(2):
                for way in range(2):
                    came = d > 0 and travels(way, h, d - 1)
                    if came:
                        got = arrived(f, way, h, d - 1)
                    if travels(way, h, d):
                        ring_copy(f, way, h, d).start()
                    if came:
                        to_mate(f, got).start()
            if d == 0:
                to_mate(f, tile_of(f, tx, ty)).start()

    def tendency(g):
        for f in range(g * GROUP, (g + 1) * GROUP):
            for b in range(per_tile):
                span = slice(b * BS, (b + 1) * BS)
                total = coupling[f : f + 1, 0:1].astype(jnp.float32) * gathered[0][here + b].astype(jnp.float32)
                for k in range(1, n_fields):
                    total = total + coupling[f : f + 1, k : k + 1].astype(jnp.float32) * gathered[k][here + b].astype(jnp.float32)
                out[f, :, span] = total

    def upstream(g):
        for f in range(g * GROUP, (g + 1) * GROUP):
            to_mate(f, column_of(f, mate)).wait_recv()
            for j in range(per_tile):
                span = slice(j * BS, (j + 1) * BS)

                first = gathered[f][picks[0, j]].astype(jnp.float32)
                second = gathered[f][picks[1, j]].astype(jnp.float32)
                w = weights[:, span].astype(jnp.float32)
                out[f, :, span] = out[f, :, span] + (w * first + (1.0 - w) * second)
            col_modes = jnp.zeros((rows, 128), jnp.float32)
            for start in range(0, cols, 2 * BS):
                span = slice(start, start + 2 * BS)
                col_modes += jnp.dot(out[f, :, span], col_b[span, :], precision=HI, preferred_element_type=jnp.float32)
            part = jnp.dot(row_bt[...], col_modes, precision=HI, preferred_element_type=jnp.float32)
            modes[g][pl.ds((f - g * GROUP) * 128, 128), :] = part
        swap_copy(g).start()

    half = GROUP * 128 // n_tx
    span_rows = half // n_ty

    def half_copy(src, dst, send, recv):
        return pltpu.make_async_remote_copy(
            src_ref=src, dst_ref=dst, send_sem=send, recv_sem=recv, device_id={"tx": mate}, device_id_type=MESH)

    def swap_copy(g):
        src = modes[g].at[pl.ds(pl.multiple_of(mate * half, 8), half), :]
        return half_copy(src, swapped[g], swap_send.at[g], swap_recv.at[g])

    def back_copy(g):
        ref = ag_bufs[g].at[pl.ds(pl.multiple_of(tx * half, 8), half), :]
        return half_copy(ref, ref, back_send.at[g], back_recv.at[g])

    def rs_copy(g, k):
        there = (ty + k) % n_ty
        return pltpu.make_async_remote_copy(
            src_ref=chip_sums[g].at[pl.ds(pl.multiple_of(there * span_rows, 8), span_rows), :], dst_ref=rs_bufs[g].at[k - 1],
            send_sem=rs_send.at[g], recv_sem=rs_recv.at[g], device_id={"ty": there}, device_id_type=MESH)

    def ag_copy(g, k):
        there = (ty + k) % n_ty
        return pltpu.make_async_remote_copy(
            src_ref=sums[g], dst_ref=ag_bufs[g].at[pl.ds(pl.multiple_of(tx * half + ty * span_rows, 8), span_rows), :],
            send_sem=ag_send.at[g], recv_sem=ag_recv.at[g], device_id={"ty": there}, device_id_type=MESH)

    def scatter(g):
        swap_copy(g).wait_recv()
        chip_sums[g][...] = modes[g][pl.ds(pl.multiple_of(tx * half, 8), half), :] + swapped[g][...]
        for k in range(1, n_ty):
            rs_copy(g, k).start()

    def reduce(g):
        whole = rs_bufs[g]
        half_copy(whole, whole, rs_send.at[g], rs_recv.at[g]).wait_recv()
        mine = chip_sums[g][pl.ds(pl.multiple_of(ty * span_rows, 8), span_rows), :]
        total = mine + jnp.sum(rs_bufs[g][...], axis=0)
        sums[g][...] = total
        for k in range(1, n_ty):
            ag_copy(g, k).start()
        ag_bufs[g][pl.ds(pl.multiple_of(tx * half + ty * span_rows, 8), span_rows), :] = total

    def hand_back(g):
        whole = rs_bufs[g]
        half_copy(whole, whole, ag_send.at[g], ag_recv.at[g]).wait_recv()
        back_copy(g).start()

    def nudge(g):
        ref = ag_bufs[g].at[pl.ds(pl.multiple_of(mate * half, 8), half), :]
        half_copy(ref, ref, back_send.at[g], back_recv.at[g]).wait_recv()
        for f in range(g * GROUP, (g + 1) * GROUP):
            coef = ag_bufs[g][pl.ds((f - g * GROUP) * 128, 128), :]
            term = relaxation[f] * (driver[f] - coef)
            recon = jnp.dot(row_b[...], term, precision=HI, preferred_element_type=jnp.float32)
            for start in range(0, cols, 2 * BS):
                span = slice(start, start + 2 * BS)
                out[f, :, span] += lax.dot_general(
                    recon, col_b[span, :], (((1,), (1,)), ((), ())), precision=HI, preferred_element_type=jnp.float32)

    stage(0, 0)
    for g in range(n_groups):
        tendency(g)
    for copy in tabs:
        copy.wait()
    end = n_groups - 1
    for g in range(end):
        behind = [upstream, scatter, reduce] if g > 0 else []
        for d in range(1, depth):
            stage(g, d)
            if behind:
                behind.pop(0)(g - 1)
        stage(g + 1, 0)
        stage(g, depth)
        if g > 0:
            for step in behind + [hand_back, nudge]:
                step(g - 1)
    for d in range(1, depth):
        stage(end, d)
        if d == 1:
            upstream(end - 1)
    scatter(end - 1)
    stage(end, depth)
    reduce(end - 1)
    upstream(end)
    scatter(end)
    hand_back(end - 1)
    reduce(end)
    nudge(end - 1)
    hand_back(end)
    nudge(end)

    for f in range(n_fields):
        sent = gathered[f].at[pl.ds(0, (n_ty - 1) * per_tile)]
        pltpu.make_async_remote_copy(
            src_ref=sent, dst_ref=sent, send_sem=ring_send.at[f], recv_sem=ring_recv.at[f, 0, 0, 0],
            device_id={"ty": toward[0]}, device_id_type=MESH).wait_send()
        to_mate(f, column_of(f, tx)).wait_send()
    for g in range(n_groups):
        swap_copy(g).wait_send()
        back_copy(g).wait_send()
        whole = rs_bufs[g]
        half_copy(whole, whole, rs_send.at[g], rs_recv.at[g]).wait_send()
        half_copy(whole, whole, ag_send.at[g], ag_recv.at[g]).wait_send()


def solution(mesh):
    n_ty, n_tx = mesh.shape["ty"], mesh.shape["tx"]
    snake = two_lines(mesh)

    def body(fields, weights, source_tile, source_block, coupling, driver, relaxation):
        n_fields, rows, cols = fields.shape
        n_groups = n_fields // GROUP
        n_dev = n_ty * n_tx
        half = GROUP * 128 // n_tx
        span_rows = half // n_ty
        row_np, col_np = wave_table(rows * n_ty), wave_table(cols * n_tx)
        row_tab, row_tab_t = jnp.asarray(row_np), jnp.asarray(np.ascontiguousarray(row_np.T))
        if row_np.shape == col_np.shape:
            col_tab = row_tab
        else:
            col_tab = jnp.asarray(col_np)
        tile = jnp.transpose(source_tile, (0, 2, 1))[0]
        block = jnp.transpose(source_block, (0, 2, 1))[0]
        picks = (tile % n_tx * n_ty + tile // n_tx) * (cols // BS) + block
        vmem = pl.BlockSpec(memory_space=pltpu.VMEM)
        smem = pl.BlockSpec(memory_space=pltpu.SMEM)
        hbm = pl.BlockSpec(memory_space=pltpu.HBM)
        dma = pltpu.SemaphoreType.DMA
        scratch = (
            [pltpu.VMEM((n_dev * (cols // BS), BS, BS), jnp.bfloat16)] * n_fields
            + [pltpu.VMEM((GROUP * 128, 128), jnp.float32)] * n_groups
            + [pltpu.VMEM((half, 128), jnp.float32)] * (2 * n_groups)
            + [pltpu.VMEM((n_ty - 1, span_rows, 128), jnp.float32)] * n_groups
            + [pltpu.VMEM((span_rows, 128), jnp.float32)] * n_groups
            + [pltpu.VMEM((GROUP * 128, 128), jnp.float32)] * n_groups
            + [
                pltpu.VMEM((rows, 128), jnp.float32),
                pltpu.VMEM((128, rows), jnp.float32),
                pltpu.VMEM((cols, 128), jnp.float32),
                pltpu.VMEM((rows, cols), jnp.bfloat16),
                pltpu.VMEM(driver.shape, jnp.float32),
                pltpu.VMEM(relaxation.shape, jnp.float32),
                dma((6,)),
                dma((n_fields, cols // BS)),
                dma((n_fields,)),
                dma((n_fields, 2, 2, n_ty // 2)),
                dma((n_fields,)),
                dma((n_fields,)),
                *[dma((n_groups,))] * 8,
            ]
        )
        return pl.pallas_call(
            functools.partial(kernel, n_ty, n_tx, snake),
            out_shape=jax.ShapeDtypeStruct((n_fields, rows, cols), jnp.float32),
            in_specs=[hbm, hbm, smem, vmem, hbm, hbm, hbm, hbm, hbm],
            out_specs=vmem,
            scratch_shapes=scratch,
            compiler_params=pltpu.CompilerParams(
                collective_id=0, has_side_effects=True, vmem_limit_bytes=67043328
            ),
            name="remap_nudge",
        )(fields, weights, picks, coupling, driver, relaxation, row_tab, row_tab_t, col_tab)

    in_specs = (
        P(None, ("groups", "ty"), "tx"),
        P(("groups", "ty"), "tx"),
        P(("groups", "ty"), "tx", None),
        P(("groups", "ty"), "tx", None),
        P(),
        P(),
        P(),
    )
    out_specs = P(None, ("groups", "ty"), "tx")
    return jax.shard_map(body, mesh=mesh, in_specs=in_specs, out_specs=out_specs, check_vma=False)
```

profile of v0, /device:TPU:1, one launch (start us, length us, event | category | flops | bytes accessed | tf_op | source)
XLA Modules:
  0.0 91.8 jit_solution(13726102177567355320)
XLA Ops:
  0.0 1.3 %bitcast_add_fusion.picks = s32[2,4]{1,0:T(2,128)} fusion(s32[1,4,2]{1,2,0:T(2,128)} %param.12, s32[1,4,2]{1,2,0:T(2,128)} %param.11), kind=kLoop, calls=%fused_computation.7 | loop fusion | flops 184 | bytes 96 | tf_op jit(solution)/shard_map/add | solution.py:292
  1.3 87.8 %remap_nudge.1 = f32[6,128,512]{2,1,0:T(8,128)} custom-call(bf16[6,128,512]{2,1,0:T(8,128)(2,1)} %fields.1, bf16[128,512]{1,0:T(8,128)(2,1)} %weights_hbm.1, s32[2,4]{1,0:T(2,128)} %bitcast_add_fusion.picks, bf16[6,6]{1,0:T(8,128)(2,1)} %coupling.1, f32[6,128,128]{2,1,0:T(8,128)} %driver_hbm.1, f32[6,128,128]{2,1,0:T(8,128)} %relaxation_hbm.1, ...), custom_call_target="tpu_custom_call" | custom-call | tf_op jit(solution)/shard_map/remap_nudge/pallas_call | solution.py:320
  89.0 2.8 %copy.11 = f32[6,128,512]{2,1,0:T(8,128)} copy(f32[6,128,512]{2,1,0:T(8,128)} %remap_nudge.1) | data formatting | bytes 3145728
where the time goes:
time: 92 us; the launch traced here: 91.8 us
  Pallas kernels  87.8 us (95%)
  local copies, waits for them, and re-layouts  2.76 us (3%)
  other arithmetic  1.27 us (1%)
    pallas_call x1, Pallas kernels, body(): pl.pallas_call(functools.partial(kernel, n_ty, n_tx, snake), out_shape=ja...  87.8 us
    unnamed x1, local copies, waits for them, and re-layouts  2.76 us

commit v1 on v0

--- a/solution.py
+++ b/solution.py
@@ -36,7 +36,7 @@
     return len(varying) > 1
 
 
-def kernel(
+def ring_kernel(
     n_ty, n_tx, snake,
     fields, weights_hbm, picks, coupling, driver_hbm, relaxation_hbm, row_tab, row_tab_t, col_tab,
     out, *scratch,
@@ -271,9 +271,504 @@
         half_copy(whole, whole, ag_send.at[g], ag_recv.at[g]).wait_send()
 
 
+def ladder(mesh):
+    devices = np.asarray(mesh.devices)
+    axis = list(mesh.axis_names).index("ty")
+    line = np.moveaxis(devices, axis, 0).reshape(devices.shape[axis], -1)[:, 0]
+    coords = [getattr(d, "coords", None) for d in line]
+    if len(line) != 8 or mesh.shape["tx"] != 2 or any(c is None for c in coords):
+        return False
+    steps = [[b - a for a, b in zip(coords[0], c)] for c in coords]
+    rung, rail = steps[1], steps[2]
+    unit = sum(abs(v) for v in rung) == 1 and sum(abs(v) for v in rail) == 1
+    return unit and all(
+        s == [k // 2 * v + k % 2 * w for v, w in zip(rail, rung)] for k, s in enumerate(steps))
+
+
+def ladder_plan(n_fields, rows):
+    chunks = [(f, 0, rows, "Q" if f % 3 == 2 else "P") for f in range(n_fields)]
+    groups = [tuple(range(f, min(f + GROUP, n_fields))) for f in range(0, n_fields, GROUP)]
+    return tuple(chunks), tuple(groups)
+
+
+def ladder_kernel(
+    n_ty, n_tx, chunks, groups,
+    fields, weights_hbm, tile_s, block_s, coupling, driver_hbm, relaxation_hbm, row_tab, row_tab_t, col_tab,
+    out, *scratch,
+):
+    n_fields, rows, cols = fields.shape
+    n_chunks, n_groups = len(chunks), len(groups)
+    gathered, asked, slots = (scratch[k * n_chunks : (k + 1) * n_chunks] for k in range(3))
+    scratch = scratch[3 * n_chunks :]
+    (modes, swapped, chip_sums, rs_bufs, sums, ag_bufs) = (
+        scratch[k * n_groups : (k + 1) * n_groups] for k in range(6))
+    (row_b, row_bt, col_b, weights, driver, relaxation, mine, rung_tile, rung_block, outer_tile, outer_block,
+     tab_sem, own_sem, mine_sem, want_send, want_recv, sent, recv, mate_send, mate_recv,
+     rs_send, rs_recv, ag_send, ag_recv, swap_send, swap_recv, back_send, back_recv) = scratch[6 * n_groups :]
+    per_tile = cols // BS
+    n_z = n_ty // 2
+    n_ask = 2 * per_tile
+    ty = lax.axis_index("ty")
+    tx = lax.axis_index("tx")
+    mate = 1 - tx
+    z, y = ty // 2, ty % 2
+    far_y = 1 - y
+    left = z < n_z // 2
+    end = (z == 0) | (z == n_z - 1)
+    inner = jnp.logical_not(end)
+    z_end = jnp.where(left, 0, n_z - 1)
+    z_in = jnp.where(left, 1, n_z - 2)
+    far_end, far_in = n_z - 1 - z_end, n_z - 1 - z_in
+    rung = 2 * z + far_y
+    across = 2 * far_in + y
+    outer = 2 * z_end + y
+    inward = 2 * z_in + y
+
+    def copy_to(src, dst, send, got, where):
+        return pltpu.make_async_remote_copy(
+            src_ref=src, dst_ref=dst, send_sem=send, recv_sem=got, device_id=where, device_id_type=MESH)
+
+    def tile(c, zz, yy, part=None, col=None):
+        first, count = ((tx if col is None else col) * n_ty + yy * n_z + zz) * per_tile, per_tile
+        if part is not None:
+            count = per_tile // 2
+            first = first + part * count
+        return gathered[c].at[pl.ds(first, count)]
+
+    def rail(c, col):
+        return gathered[c].at[pl.ds((col * n_ty + y * n_z) * per_tile, n_z * per_tile)]
+
+    def column(c, col):
+        return gathered[c].at[pl.ds(col * n_ty * per_tile, n_ty * per_tile)]
+
+    def send(c, ref, there, kind):
+        copy_to(ref, ref, sent.at[c], recv.at[c, kind], {"ty": there}).start()
+
+    def take(c, ref, kind):
+        copy_to(ref, ref, sent.at[c], recv.at[c, kind], {"ty": rung}).wait_recv()
+
+    def to_mate(c, ref):
+        return copy_to(ref, ref, mate_send.at[c], mate_recv.at[c], {"tx": mate})
+
+    E_OWN, E_FAR, I_ACROSS, E_ACROSS, I_PART, OWN_RUNG, E_RUNG, I_REST, ASKED = range(9)
+
+    tabs = [
+        pltpu.make_async_copy(row_tab.at[pl.ds(ty * rows, rows), :], row_b, tab_sem.at[0]),
+        pltpu.make_async_copy(row_tab_t.at[:, pl.ds(pl.multiple_of(ty * rows, 128), rows)], row_bt, tab_sem.at[1]),
+        pltpu.make_async_copy(col_tab.at[pl.ds(tx * cols, cols), :], col_b, tab_sem.at[2]),
+        pltpu.make_async_copy(weights_hbm, weights, tab_sem.at[3]),
+        pltpu.make_async_copy(driver_hbm, driver, tab_sem.at[4]),
+        pltpu.make_async_copy(relaxation_hbm, relaxation, tab_sem.at[5]),
+    ]
+
+    barrier = pltpu.get_barrier_semaphore()
+    pl.semaphore_signal(barrier, inc=1, device_id={"tx": mate}, device_id_type=MESH)
+    for k in range(1, n_ty):
+        pl.semaphore_signal(barrier, inc=1, device_id={"ty": (ty + k) % n_ty}, device_id_type=MESH)
+    here = (tx * n_ty + y * n_z + z) * per_tile
+    own = [
+        [pltpu.make_async_copy(fields.at[f, pl.ds(r0, nr), pl.ds(b * BS, BS)], gathered[c].at[here + b], own_sem.at[c, b])
+         for b in range(per_tile)]
+        for c, (f, r0, nr, _) in enumerate(chunks)
+    ]
+    mine_copy = pltpu.make_async_copy(fields, mine, mine_sem)
+    for copies in own:
+        for copy in copies:
+            copy.start()
+    for copy in [mine_copy] + tabs:
+        copy.start()
+    pl.semaphore_wait(barrier, n_ty)
+
+    want = [
+        (copy_to(tile_s, rung_tile, want_send.at[0], want_recv.at[0], {"ty": rung}),
+         copy_to(block_s, rung_block, want_send.at[1], want_recv.at[1], {"ty": rung})),
+        (copy_to(tile_s, outer_tile, want_send.at[2], want_recv.at[2], {"ty": inward}),
+         copy_to(block_s, outer_block, want_send.at[3], want_recv.at[3], {"ty": inward})),
+    ]
+    for copy in want[0]:
+        copy.start()
+
+    @pl.when(end)
+    def _():
+        for copy in want[1]:
+            copy.start()
+
+    def spot(tiles, blocks, s, j):
+        t = tiles[s, j]
+        row, col = lax.div(t, n_tx), lax.rem(t, n_tx)
+        row_z, row_y = lax.div(row, 2), lax.rem(row, 2)
+        return col, row_z, row_y, blocks[s, j]
+
+    def place(col, row_z, row_y, block):
+        return (col * n_ty + row_y * n_z + row_z) * per_tile + block
+
+    def launch(c):
+        for copy in own[c]:
+            copy.wait()
+        ref = tile(c, z, y)
+        if chunks[c][3] == "P":
+            @pl.when(inner)
+            def _():
+                send(c, ref, rung, OWN_RUNG)
+                send(c, ref, across, I_ACROSS)
+                to_mate(c, ref).start()
+
+            @pl.when(end)
+            def _():
+                send(c, ref, rung, OWN_RUNG)
+                send(c, ref, inward, E_OWN)
+        else:
+            @pl.when(inner)
+            def _():
+                send(c, ref, across, I_ACROSS)
+                send(c, ref, outer, E_OWN)
+
+            @pl.when(end)
+            def _():
+                send(c, ref, inward, E_OWN)
+            to_mate(c, ref).start()
+
+    def first_hop(c):
+        if chunks[c][3] == "P":
+            @pl.when(inner)
+            def _():
+                ref = tile(c, z_end, y)
+                take(c, ref, E_OWN)
+                send(c, ref, across, E_ACROSS)
+                to_mate(c, ref).start()
+                ref = tile(c, z, far_y)
+                take(c, ref, OWN_RUNG)
+                send(c, tile(c, z, far_y, 0), across, I_PART)
+                to_mate(c, ref).start()
+                ref = tile(c, far_in, y)
+                take(c, ref, I_ACROSS)
+                send(c, tile(c, far_in, y, 1), rung, I_REST)
+                to_mate(c, ref).start()
+
+            @pl.when(end)
+            def _():
+                ref = tile(c, z, far_y)
+                take(c, ref, OWN_RUNG)
+                send(c, ref, inward, E_FAR)
+        else:
+            @pl.when(inner)
+            def _():
+                ref = tile(c, z_end, y)
+                take(c, ref, E_OWN)
+                send(c, ref, across, E_ACROSS)
+                to_mate(c, ref).start()
+                ref = tile(c, far_in, y)
+                take(c, ref, I_ACROSS)
+                send(c, ref, outer, I_ACROSS)
+                to_mate(c, ref).start()
+
+            @pl.when(end)
+            def _():
+                ref = tile(c, z_in, y)
+                take(c, ref, E_OWN)
+                to_mate(c, ref).start()
+
+    def second_hop(c):
+        if chunks[c][3] == "P":
+            @pl.when(inner)
+            def _():
+                ref = tile(c, far_end, y)
+                take(c, ref, E_ACROSS)
+                send(c, ref, rung, E_RUNG)
+                to_mate(c, ref).start()
+                ref = tile(c, z_end, far_y)
+                take(c, ref, E_FAR)
+                to_mate(c, ref).start()
+        else:
+            @pl.when(inner)
+            def _():
+                ref = tile(c, far_end, y)
+                take(c, ref, E_ACROSS)
+                send(c, ref, outer, E_ACROSS)
+                to_mate(c, ref).start()
+
+            @pl.when(end)
+            def _():
+                ref = tile(c, far_in, y)
+                take(c, ref, I_ACROSS)
+                to_mate(c, ref).start()
+
+    def answer(c):
+        if chunks[c][3] == "P":
+            @pl.when(inner)
+            def _():
+                take(c, tile(c, far_in, far_y, 0), I_PART)
+                take(c, tile(c, far_in, far_y, 1), I_REST)
+                to_mate(c, tile(c, far_in, far_y)).start()
+                ref = tile(c, far_end, far_y)
+                take(c, ref, E_RUNG)
+                to_mate(c, ref).start()
+                to_mate(c, column(c, mate)).wait_recv()
+                for s in range(2):
+                    for j in range(per_tile):
+                        col, row_z, row_y, block = spot(outer_tile, outer_block, s, j)
+                        asked[c][s * per_tile + j] = gathered[c][place(col, row_z, row_y, block)]
+                copy_to(asked[c], slots[c], sent.at[c], recv.at[c, ASKED], {"ty": outer}).start()
+        else:
+            @pl.when(end)
+            def _():
+                ref = tile(c, far_end, y)
+                take(c, ref, E_ACROSS)
+                to_mate(c, ref).start()
+            to_mate(c, rail(c, mate)).wait_recv()
+            for s in range(2):
+                for j in range(per_tile):
+                    col, row_z, row_y, block = spot(rung_tile, rung_block, s, j)
+                    asked[c][s * per_tile + j] = gathered[c][place(col, row_z, y, block)]
+            copy_to(asked[c], slots[c], sent.at[c], recv.at[c, ASKED], {"ty": rung}).start()
+
+    def blend(c):
+        f, r0, nr, mode = chunks[c]
+        whole = copy_to(asked[c], slots[c], sent.at[c], recv.at[c, ASKED], {"ty": rung})
+        if mode == "P":
+            @pl.when(end)
+            def _():
+                whole.wait_recv()
+        else:
+            whole.wait_recv()
+
+        def source(s, j):
+            col, row_z, row_y, block = spot(tile_s, block_s, s, j)
+            if mode == "P":
+                here_too = inner
+                at = place(col, row_z, row_y, block)
+            else:
+                here_too = row_y == y
+                at = place(col, row_z, y, block)
+            return jnp.where(here_too, gathered[c][at].astype(jnp.float32), slots[c][s * per_tile + j].astype(jnp.float32))
+
+        for j in range(per_tile):
+            span = slice(j * BS, (j + 1) * BS)
+            w = weights[r0 : r0 + nr, span].astype(jnp.float32)
+            out[f, r0 : r0 + nr, span] = out[f, r0 : r0 + nr, span] + (w * source(0, j) + (1.0 - w) * source(1, j))
+
+    def tendency(f):
+        for b in range(per_tile):
+            span = slice(b * BS, (b + 1) * BS)
+            total = coupling[f : f + 1, 0:1].astype(jnp.float32) * mine[0, :, span].astype(jnp.float32)
+            for k in range(1, n_fields):
+                total = total + coupling[f : f + 1, k : k + 1].astype(jnp.float32) * mine[k, :, span].astype(jnp.float32)
+            out[f, :, span] = total
+
+    def project(g, f):
+        col_modes = jnp.zeros((rows, 128), jnp.float32)
+        for start in range(0, cols, 2 * BS):
+            span = slice(start, start + 2 * BS)
+            col_modes += jnp.dot(out[f, :, span], col_b[span, :], precision=HI, preferred_element_type=jnp.float32)
+        part = jnp.dot(row_bt[...], col_modes, precision=HI, preferred_element_type=jnp.float32)
+        modes[g][pl.ds((f - groups[g][0]) * 128, 128), :] = part
+        if f == groups[g][-1]:
+            swap_copy(g).start()
+
+    def sizes(g):
+        half = len(groups[g]) * 128 // n_tx
+        return half, half // n_ty
+
+    def swap_copy(g):
+        half, _ = sizes(g)
+        src = modes[g].at[pl.ds(pl.multiple_of(mate * half, 8), half), :]
+        return copy_to(src, swapped[g], swap_send.at[g], swap_recv.at[g], {"tx": mate})
+
+    def back_copy(g):
+        half, _ = sizes(g)
+        ref = ag_bufs[g].at[pl.ds(pl.multiple_of(tx * half, 8), half), :]
+        return copy_to(ref, ref, back_send.at[g], back_recv.at[g], {"tx": mate})
+
+    def rs_copy(g, k):
+        _, span_rows = sizes(g)
+        there = (ty + k) % n_ty
+        src = chip_sums[g].at[pl.ds(pl.multiple_of(there * span_rows, 8), span_rows), :]
+        return copy_to(src, rs_bufs[g].at[k - 1], rs_send.at[g], rs_recv.at[g], {"ty": there})
+
+    def ag_copy(g, k):
+        half, span_rows = sizes(g)
+        there = (ty + k) % n_ty
+        dst = ag_bufs[g].at[pl.ds(pl.multiple_of(tx * half + ty * span_rows, 8), span_rows), :]
+        return copy_to(sums[g], dst, ag_send.at[g], ag_recv.at[g], {"ty": there})
+
+    def scatter(g):
+        half, _ = sizes(g)
+        swap_copy(g).wait_recv()
+        chip_sums[g][...] = modes[g][pl.ds(pl.multiple_of(tx * half, 8), half), :] + swapped[g][...]
+        for k in range(1, n_ty):
+            rs_copy(g, k).start()
+
+    def reduce(g):
+        half, span_rows = sizes(g)
+        whole = rs_bufs[g]
+        copy_to(whole, whole, rs_send.at[g], rs_recv.at[g], {"tx": mate}).wait_recv()
+        part = chip_sums[g][pl.ds(pl.multiple_of(ty * span_rows, 8), span_rows), :]
+        total = part + jnp.sum(rs_bufs[g][...], axis=0)
+        sums[g][...] = total
+        for k in range(1, n_ty):
+            ag_copy(g, k).start()
+        ag_bufs[g][pl.ds(pl.multiple_of(tx * half + ty * span_rows, 8), span_rows), :] = total
+
+    def hand_back(g):
+        whole = rs_bufs[g]
+        copy_to(whole, whole, ag_send.at[g], ag_recv.at[g], {"tx": mate}).wait_recv()
+        back_copy(g).start()
+
+    def nudge(g):
+        half, _ = sizes(g)
+        ref = ag_bufs[g].at[pl.ds(pl.multiple_of(mate * half, 8), half), :]
+        copy_to(ref, ref, back_send.at[g], back_recv.at[g], {"tx": mate}).wait_recv()
+        for f in groups[g]:
+            coef = ag_bufs[g][pl.ds((f - groups[g][0]) * 128, 128), :]
+            term = relaxation[f] * (driver[f] - coef)
+            recon = jnp.dot(row_b[...], term, precision=HI, preferred_element_type=jnp.float32)
+            for start in range(0, cols, 2 * BS):
+                span = slice(start, start + 2 * BS)
+                out[f, :, span] += lax.dot_general(
+                    recon, col_b[span, :], (((1,), (1,)), ((), ())), precision=HI, preferred_element_type=jnp.float32)
+
+    last_chunk = {f: c for c, (f, _, _, _) in enumerate(chunks)}
+    group_of = {f: g for g, fs in enumerate(groups) for f in fs}
+    todo = []
+
+    def work(count=1):
+        for _ in range(min(count, len(todo))):
+            step, g = todo.pop(0)
+            step(g)
+
+    def finish(c):
+        blend(c)
+        f = chunks[c][0]
+        if last_chunk[f] == c:
+            g = group_of[f]
+            project(g, f)
+            if f == groups[g][-1]:
+                todo.extend([(scatter, g), (reduce, g), (hand_back, g), (nudge, g)])
+
+    launch(0)
+    mine_copy.wait()
+    fresh = list(range(n_fields))
+    launch(1)
+    tendency(fresh.pop(0))
+    for k in range(n_chunks + 2):
+        if 0 < k and k + 1 < n_chunks:
+            launch(k + 1)
+        if k < n_chunks:
+            first_hop(k)
+        if fresh:
+            tendency(fresh.pop(0))
+        if k == 1:
+            for copy in tabs:
+                copy.wait()
+            for copy in want[0]:
+                copy.wait_recv()
+
+            @pl.when(inner)
+            def _():
+                for copy in want[1]:
+                    copy.wait_recv()
+        if 0 <= k - 2:
+            work(1)
+            finish(k - 2)
+        if 0 <= k - 1 < n_chunks:
+            answer(k - 1)
+            work(1)
+        if k < n_chunks:
+            second_hop(k)
+    while todo:
+        work(1)
+
+    for c in range(n_chunks):
+        mode = chunks[c][3]
+
+        @pl.when(inner)
+        def _():
+            ref = gathered[c].at[pl.ds(0, 7 * per_tile)]
+            copy_to(ref, ref, sent.at[c], recv.at[c, 0], {"ty": rung}).wait_send()
+            if mode == "P":
+                to_mate(c, column(c, tx)).wait_send()
+
+        @pl.when(end)
+        def _():
+            ref = gathered[c].at[pl.ds(0, 3 * per_tile)]
+            copy_to(ref, ref, sent.at[c], recv.at[c, 0], {"ty": rung}).wait_send()
+
+        if mode == "Q":
+            to_mate(c, rail(c, tx)).wait_send()
+    for copy in want[0]:
+        copy.wait_send()
+
+    @pl.when(end)
+    def _():
+        for copy in want[1]:
+            copy.wait_send()
+    for g in range(n_groups):
+        swap_copy(g).wait_send()
+        back_copy(g).wait_send()
+        whole = rs_bufs[g]
+        copy_to(whole, whole, rs_send.at[g], rs_recv.at[g], {"tx": mate}).wait_send()
+        copy_to(whole, whole, ag_send.at[g], ag_recv.at[g], {"tx": mate}).wait_send()
+
+
+def ladder_call(
+    n_ty, n_tx, fields, weights, tile, block, coupling, driver, relaxation, row_tab, row_tab_t, col_tab,
+):
+    n_fields, rows, cols = fields.shape
+    chunks, groups = ladder_plan(n_fields, rows)
+    n_chunks, n_groups = len(chunks), len(groups)
+    per_tile = cols // BS
+    vmem = pl.BlockSpec(memory_space=pltpu.VMEM)
+    smem = pl.BlockSpec(memory_space=pltpu.SMEM)
+    hbm = pl.BlockSpec(memory_space=pltpu.HBM)
+    dma = pltpu.SemaphoreType.DMA
+    halves = [len(g) * 128 // n_tx for g in groups]
+    asks = pltpu.SMEM((2, per_tile), jnp.int32)
+    scratch = (
+        [pltpu.VMEM((n_ty * n_tx * per_tile, c[2], BS), jnp.bfloat16) for c in chunks]
+        + [pltpu.VMEM((2 * per_tile, c[2], BS), jnp.bfloat16) for c in chunks] * 2
+        + [pltpu.VMEM((len(g) * 128, 128), jnp.float32) for g in groups]
+        + [pltpu.VMEM((h, 128), jnp.float32) for h in halves] * 2
+        + [pltpu.VMEM((n_ty - 1, h // n_ty, 128), jnp.float32) for h in halves]
+        + [pltpu.VMEM((h // n_ty, 128), jnp.float32) for h in halves]
+        + [pltpu.VMEM((len(g) * 128, 128), jnp.float32) for g in groups]
+        + [
+            pltpu.VMEM((rows, 128), jnp.float32),
+            pltpu.VMEM((128, rows), jnp.float32),
+            pltpu.VMEM((cols, 128), jnp.float32),
+            pltpu.VMEM((rows, cols), jnp.bfloat16),
+            pltpu.VMEM(driver.shape, jnp.float32),
+            pltpu.VMEM(relaxation.shape, jnp.float32),
+            pltpu.VMEM(fields.shape, jnp.bfloat16),
+            asks, asks, asks, asks,
+            dma((6,)),
+            dma((n_chunks, per_tile)),
+            dma,
+            dma((4,)),
+            dma((4,)),
+            dma((n_chunks,)),
+            dma((n_chunks, 9)),
+            dma((n_chunks,)),
+            dma((n_chunks,)),
+            *[dma((n_groups,))] * 8,
+        ]
+    )
+    return pl.pallas_call(
+        functools.partial(ladder_kernel, n_ty, n_tx, chunks, groups),
+        out_shape=jax.ShapeDtypeStruct((n_fields, rows, cols), jnp.float32),
+        in_specs=[hbm, hbm, smem, smem, vmem, hbm, hbm, hbm, hbm, hbm],
+        out_specs=vmem,
+        scratch_shapes=scratch,
+        compiler_params=pltpu.CompilerParams(
+            collective_id=0, has_side_effects=True, vmem_limit_bytes=67043328
+        ),
+        name="remap_ladder",
+    )(fields, weights, tile, block, coupling, driver, relaxation, row_tab, row_tab_t, col_tab)
+
+
 def solution(mesh):
     n_ty, n_tx = mesh.shape["ty"], mesh.shape["tx"]
     snake = two_lines(mesh)
+    rungs = ladder(mesh)
 
     def body(fields, weights, source_tile, source_block, coupling, driver, relaxation):
         n_fields, rows, cols = fields.shape
@@ -289,6 +784,9 @@
             col_tab = jnp.asarray(col_np)
         tile = jnp.transpose(source_tile, (0, 2, 1))[0]
         block = jnp.transpose(source_block, (0, 2, 1))[0]
+        if rungs:
+            return ladder_call(
+                n_ty, n_tx, fields, weights, tile, block, coupling, driver, relaxation, row_tab, row_tab_t, col_tab)
         picks = (tile % n_tx * n_ty + tile // n_tx) * (cols // BS) + block
         vmem = pl.BlockSpec(memory_space=pltpu.VMEM)
         smem = pl.BlockSpec(memory_space=pltpu.SMEM)
@@ -318,7 +816,7 @@
             ]
         )
         return pl.pallas_call(
-            functools.partial(kernel, n_ty, n_tx, snake),
+            functools.partial(ring_kernel, n_ty, n_tx, snake),
             out_shape=jax.ShapeDtypeStruct((n_fields, rows, cols), jnp.float32),
             in_specs=[hbm, hbm, smem, vmem, hbm, hbm, hbm, hbm, hbm],
             out_specs=vmem,

time: 92 us -> 95.9 us (1.042)
  Pallas kernels: 87.8 us -> 92.9 us
  other arithmetic: 1.27 us -> 0 us
    pallas_call x1, Pallas kernels: 87.8 us -> 92.9 us  [ladder_call(): pl.pallas_call(functools.partial(ladder_kernel, n_ty, n_tx, chunks, group...]
    add x1 -> x0, other arithmetic: 1.27 us -> none  [body(): picks = (tile % n_tx * n_ty + tile // n_tx) * (cols // BS) + block]
where the time goes in v1:
time: 95.9 us; the launch traced here: 95.7 us
  Pallas kernels  92.9 us (97%)
  local copies, waits for them, and re-layouts  2.76 us (3%)
    pallas_call x1, Pallas kernels, ladder_call(): pl.pallas_call(functools.partial(ladder_kernel, n_ty, n_tx, chunks, group...  92.9 us
    unnamed x1, local copies, waits for them, and re-layouts  2.76 us

profile of v1, /device:TPU:1, one launch (start us, length us, event | category | flops | bytes accessed | tf_op | source)
XLA Modules:
  0.0 95.7 jit_solution(5291539881108537460)
XLA Ops:
  0.0 92.9 %remap_ladder.1 = f32[6,128,512]{2,1,0:T(8,128)} custom-call(bf16[6,128,512]{2,1,0:T(8,128)(2,1)} %fields.1, bf16[128,512]{1,0:T(8,128)(2,1)} %weights_hbm.1, s32[2,4]{1,0:T(2,128)} %bitcast.6, s32[2,4]{1,0:T(2,128)} %bitcast.7, bf16[6,6]{1,0:T(8,128)(2,1)} %coupling.1, f32[6,128,128]{2,1,0:T(8,128)} %driver_hbm.1, f32[6,128,128]{2,1,0:T(8,128)} %relaxation_hbm.1, ...), custom_call_target="tpu_custom_call" | custom-call | tf_op jit(solution)/shard_map/remap_ladder/pallas_call | solution.py:755
  92.9 2.8 %copy.11 = f32[6,128,512]{2,1,0:T(8,128)} copy(f32[6,128,512]{2,1,0:T(8,128)} %remap_ladder.1) | data formatting | bytes 3145728

commit v2 on v1

--- a/solution.py
+++ b/solution.py
@@ -285,8 +285,17 @@
         s == [k // 2 * v + k % 2 * w for v, w in zip(rail, rung)] for k, s in enumerate(steps))
 
 
+SPLIT = 2
+PATTERN = "QPP"
+LAUNCH, SECOND, COLLECT, ANSWER, FINISH = 3, 1, 2, 3, 5
+ADDS = (1, 2, 2, 2)
+
+
 def ladder_plan(n_fields, rows):
-    chunks = [(f, 0, rows, "Q" if f % 3 == 2 else "P") for f in range(n_fields)]
+    pieces = SPLIT if rows % (16 * SPLIT) == 0 else 1
+    size = rows // pieces
+    spots = [(f, r) for f in range(n_fields) for r in range(0, rows, size)]
+    chunks = [(f, r, size, PATTERN[k % len(PATTERN)]) for k, (f, r) in enumerate(spots)]
     groups = [tuple(range(f, min(f + GROUP, n_fields))) for f in range(0, n_fields, GROUP)]
     return tuple(chunks), tuple(groups)
 
@@ -493,7 +502,7 @@
                 take(c, ref, I_ACROSS)
                 to_mate(c, ref).start()
 
-    def answer(c):
+    def collect(c):
         if chunks[c][3] == "P":
             @pl.when(inner)
             def _():
@@ -503,6 +512,17 @@
                 ref = tile(c, far_end, far_y)
                 take(c, ref, E_RUNG)
                 to_mate(c, ref).start()
+        else:
+            @pl.when(end)
+            def _():
+                ref = tile(c, far_end, y)
+                take(c, ref, E_ACROSS)
+                to_mate(c, ref).start()
+
+    def answer(c):
+        if chunks[c][3] == "P":
+            @pl.when(inner)
+            def _():
                 to_mate(c, column(c, mate)).wait_recv()
                 for s in range(2):
                     for j in range(per_tile):
@@ -510,11 +530,6 @@
                         asked[c][s * per_tile + j] = gathered[c][place(col, row_z, row_y, block)]
                 copy_to(asked[c], slots[c], sent.at[c], recv.at[c, ASKED], {"ty": outer}).start()
         else:
-            @pl.when(end)
-            def _():
-                ref = tile(c, far_end, y)
-                take(c, ref, E_ACROSS)
-                to_mate(c, ref).start()
             to_mate(c, rail(c, mate)).wait_recv()
             for s in range(2):
                 for j in range(per_tile):
@@ -629,34 +644,29 @@
 
     last_chunk = {f: c for c, (f, _, _, _) in enumerate(chunks)}
     group_of = {f: g for g, fs in enumerate(groups) for f in fs}
-    todo = []
-
-    def work(count=1):
-        for _ in range(min(count, len(todo))):
-            step, g = todo.pop(0)
-            step(g)
-
-    def finish(c):
+    todo = {}
+
+    def finish(c, k):
         blend(c)
         f = chunks[c][0]
         if last_chunk[f] == c:
             g = group_of[f]
             project(g, f)
             if f == groups[g][-1]:
-                todo.extend([(scatter, g), (reduce, g), (hand_back, g), (nudge, g)])
-
-    launch(0)
+                due = k
+                for step, gap in zip((scatter, reduce, hand_back, nudge), ADDS):
+                    due += gap
+                    todo.setdefault(due, []).append((step, g))
+
+    started = 0
+    while started < min(LAUNCH, n_chunks):
+        launch(started)
+        started += 1
     mine_copy.wait()
     fresh = list(range(n_fields))
-    launch(1)
     tendency(fresh.pop(0))
-    for k in range(n_chunks + 2):
-        if 0 < k and k + 1 < n_chunks:
-            launch(k + 1)
-        if k < n_chunks:
-            first_hop(k)
-        if fresh:
-            tendency(fresh.pop(0))
+    k = 0
+    while k < n_chunks + FINISH or todo:
         if k == 1:
             for copy in tabs:
                 copy.wait()
@@ -667,16 +677,24 @@
             def _():
                 for copy in want[1]:
                     copy.wait_recv()
-        if 0 <= k - 2:
-            work(1)
-            finish(k - 2)
-        if 0 <= k - 1 < n_chunks:
-            answer(k - 1)
-            work(1)
         if k < n_chunks:
-            second_hop(k)
-    while todo:
-        work(1)
+            first_hop(k)
+        if started < n_chunks:
+            launch(started)
+            started += 1
+        if 0 <= k - SECOND < n_chunks:
+            second_hop(k - SECOND)
+        if 0 <= k - COLLECT < n_chunks:
+            collect(k - COLLECT)
+        if 0 <= k - ANSWER < n_chunks:
+            answer(k - ANSWER)
+        if fresh:
+            tendency(fresh.pop(0))
+        for step, g in todo.pop(k, ()):
+            step(g)
+        if 0 <= k - FINISH < n_chunks:
+            finish(k - FINISH, k)
+        k += 1
 
     for c in range(n_chunks):
         mode = chunks[c][3]

time: 95.9 us -> 79.5 us (0.83)
  Pallas kernels: 92.9 us -> 76.5 us
    pallas_call x1, Pallas kernels: 92.9 us -> 76.5 us  [ladder_call(): pl.pallas_call(functools.partial(ladder_kernel, n_ty, n_tx, chunks, group...]
where the time goes in v2:
time: 79.5 us; the launch traced here: 79.3 us
  Pallas kernels  76.5 us (96%)
  local copies, waits for them, and re-layouts  2.76 us (3%)
    pallas_call x1, Pallas kernels, ladder_call(): pl.pallas_call(functools.partial(ladder_kernel, n_ty, n_tx, chunks, group...  76.5 us
    unnamed x1, local copies, waits for them, and re-layouts  2.76 us

profile of v2, /device:TPU:1, one launch (start us, length us, event | category | flops | bytes accessed | tf_op | source)
XLA Modules:
  0.0 79.3 jit_solution(11439275849326011772)
XLA Ops:
  0.0 76.5 %remap_ladder.1 = f32[6,128,512]{2,1,0:T(8,128)} custom-call(bf16[6,128,512]{2,1,0:T(8,128)(2,1)} %fields.1, bf16[128,512]{1,0:T(8,128)(2,1)} %weights_hbm.1, s32[2,4]{1,0:T(2,128)} %bitcast.6, s32[2,4]{1,0:T(2,128)} %bitcast.7, bf16[6,6]{1,0:T(8,128)(2,1)} %coupling.1, f32[6,128,128]{2,1,0:T(8,128)} %driver_hbm.1, f32[6,128,128]{2,1,0:T(8,128)} %relaxation_hbm.1, ...), custom_call_target="tpu_custom_call" | custom-call | tf_op jit(solution)/shard_map/remap_ladder/pallas_call | solution.py:773
  76.6 2.8 %copy.11 = f32[6,128,512]{2,1,0:T(8,128)} copy(f32[6,128,512]{2,1,0:T(8,128)} %remap_ladder.1) | data formatting | bytes 3145728

commit v3 on v2

--- a/solution.py
+++ b/solution.py
@@ -286,9 +286,10 @@
 
 
 SPLIT = 2
-PATTERN = "QPP"
+PATTERN = "PQPPQPPQPPQP"
 LAUNCH, SECOND, COLLECT, ANSWER, FINISH = 3, 1, 2, 3, 5
-ADDS = (1, 2, 2, 2)
+ADDS = ((1, 2, 1, 1), (1, 3))
+GROUPS = (5, 1)
 
 
 def ladder_plan(n_fields, rows):
@@ -296,7 +297,9 @@
     size = rows // pieces
     spots = [(f, r) for f in range(n_fields) for r in range(0, rows, size)]
     chunks = [(f, r, size, PATTERN[k % len(PATTERN)]) for k, (f, r) in enumerate(spots)]
-    groups = [tuple(range(f, min(f + GROUP, n_fields))) for f in range(0, n_fields, GROUP)]
+    counts = GROUPS if sum(GROUPS) == n_fields else (1,) * n_fields
+    ends = [sum(counts[: k + 1]) for k in range(len(counts))]
+    groups = [tuple(range(e - n, e)) for e, n in zip(ends, counts)]
     return tuple(chunks), tuple(groups)
 
 
@@ -372,8 +375,16 @@
 
     barrier = pltpu.get_barrier_semaphore()
     pl.semaphore_signal(barrier, inc=1, device_id={"tx": mate}, device_id_type=MESH)
-    for k in range(1, n_ty):
-        pl.semaphore_signal(barrier, inc=1, device_id={"ty": (ty + k) % n_ty}, device_id_type=MESH)
+    pl.semaphore_signal(barrier, inc=1, device_id={"ty": rung}, device_id_type=MESH)
+
+    @pl.when(inner)
+    def _():
+        pl.semaphore_signal(barrier, inc=1, device_id={"ty": across}, device_id_type=MESH)
+        pl.semaphore_signal(barrier, inc=1, device_id={"ty": outer}, device_id_type=MESH)
+
+    @pl.when(end)
+    def _():
+        pl.semaphore_signal(barrier, inc=1, device_id={"ty": inward}, device_id_type=MESH)
     here = (tx * n_ty + y * n_z + z) * per_tile
     own = [
         [pltpu.make_async_copy(fields.at[f, pl.ds(r0, nr), pl.ds(b * BS, BS)], gathered[c].at[here + b], own_sem.at[c, b])
@@ -386,7 +397,14 @@
             copy.start()
     for copy in [mine_copy] + tabs:
         copy.start()
-    pl.semaphore_wait(barrier, n_ty)
+
+    @pl.when(inner)
+    def _():
+        pl.semaphore_wait(barrier, 4)
+
+    @pl.when(end)
+    def _():
+        pl.semaphore_wait(barrier, 3)
 
     want = [
         (copy_to(tile_s, rung_tile, want_send.at[0], want_recv.at[0], {"ty": rung}),
@@ -578,33 +596,39 @@
         part = jnp.dot(row_bt[...], col_modes, precision=HI, preferred_element_type=jnp.float32)
         modes[g][pl.ds((f - groups[g][0]) * 128, 128), :] = part
         if f == groups[g][-1]:
-            swap_copy(g).start()
+            if g in direct:
+                spread(g)
+            else:
+                swap_copy(g).start()
+
+    direct = (n_groups - 1,)
 
     def sizes(g):
         half = len(groups[g]) * 128 // n_tx
         return half, half // n_ty
 
+    def rows_of(ref, first, count):
+        return ref.at[pl.ds(pl.multiple_of(first, 8), count), :]
+
     def swap_copy(g):
         half, _ = sizes(g)
-        src = modes[g].at[pl.ds(pl.multiple_of(mate * half, 8), half), :]
-        return copy_to(src, swapped[g], swap_send.at[g], swap_recv.at[g], {"tx": mate})
+        return copy_to(rows_of(modes[g], mate * half, half), swapped[g], swap_send.at[g], swap_recv.at[g], {"tx": mate})
 
     def back_copy(g):
         half, _ = sizes(g)
-        ref = ag_bufs[g].at[pl.ds(pl.multiple_of(tx * half, 8), half), :]
+        ref = rows_of(ag_bufs[g], tx * half, half)
         return copy_to(ref, ref, back_send.at[g], back_recv.at[g], {"tx": mate})
 
     def rs_copy(g, k):
-        _, span_rows = sizes(g)
+        _, span = sizes(g)
         there = (ty + k) % n_ty
-        src = chip_sums[g].at[pl.ds(pl.multiple_of(there * span_rows, 8), span_rows), :]
+        src = rows_of(chip_sums[g], there * span, span)
         return copy_to(src, rs_bufs[g].at[k - 1], rs_send.at[g], rs_recv.at[g], {"ty": there})
 
     def ag_copy(g, k):
-        half, span_rows = sizes(g)
-        there = (ty + k) % n_ty
-        dst = ag_bufs[g].at[pl.ds(pl.multiple_of(tx * half + ty * span_rows, 8), span_rows), :]
-        return copy_to(sums[g], dst, ag_send.at[g], ag_recv.at[g], {"ty": there})
+        half, span = sizes(g)
+        dst = rows_of(ag_bufs[g], tx * half + ty * span, span)
+        return copy_to(sums[g], dst, ag_send.at[g], ag_recv.at[g], {"ty": (ty + k) % n_ty})
 
     def scatter(g):
         half, _ = sizes(g)
@@ -614,15 +638,14 @@
             rs_copy(g, k).start()
 
     def reduce(g):
-        half, span_rows = sizes(g)
+        half, span = sizes(g)
         whole = rs_bufs[g]
         copy_to(whole, whole, rs_send.at[g], rs_recv.at[g], {"tx": mate}).wait_recv()
-        part = chip_sums[g][pl.ds(pl.multiple_of(ty * span_rows, 8), span_rows), :]
-        total = part + jnp.sum(rs_bufs[g][...], axis=0)
+        total = chip_sums[g][pl.ds(pl.multiple_of(ty * span, 8), span), :] + jnp.sum(rs_bufs[g][...], axis=0)
         sums[g][...] = total
         for k in range(1, n_ty):
             ag_copy(g, k).start()
-        ag_bufs[g][pl.ds(pl.multiple_of(tx * half + ty * span_rows, 8), span_rows), :] = total
+        ag_bufs[g][pl.ds(pl.multiple_of(tx * half + ty * span, 8), span), :] = total
 
     def hand_back(g):
         whole = rs_bufs[g]
@@ -631,8 +654,11 @@
 
     def nudge(g):
         half, _ = sizes(g)
-        ref = ag_bufs[g].at[pl.ds(pl.multiple_of(mate * half, 8), half), :]
+        ref = rows_of(ag_bufs[g], mate * half, half)
         copy_to(ref, ref, back_send.at[g], back_recv.at[g], {"tx": mate}).wait_recv()
+        correct(g)
+
+    def correct(g):
         for f in groups[g]:
             coef = ag_bufs[g][pl.ds((f - groups[g][0]) * 128, 128), :]
             term = relaxation[f] * (driver[f] - coef)
@@ -642,6 +668,66 @@
                 out[f, :, span] += lax.dot_general(
                     recon, col_b[span, :], (((1,), (1,)), ((), ())), precision=HI, preferred_element_type=jnp.float32)
 
+    n_own = n_ty * n_tx // 2
+
+    def relations():
+        for dz in range(2):
+            for dy in range(2):
+                for dt in range(2):
+                    yield dz * 4 + dy * 2 + dt, (z_in, far_in)[dz], (z_end, far_end)[dz], (y, far_y)[dy], (tx, mate)[dt]
+
+    def owner_rows(g, zz, yy, tt):
+        span = len(groups[g]) * 128 // n_own
+        return ((zz - 1) * 4 + yy * 2 + tt) * span, span
+
+    def spread_copy(g, slot, zz, yy, tt):
+        src = rows_of(modes[g], *owner_rows(g, zz, yy, tt))
+        return copy_to(src, rs_bufs[g].at[slot], rs_send.at[g], rs_recv.at[g], {"ty": 2 * zz + yy, "tx": tt})
+
+    def spread(g):
+        @pl.when(inner)
+        def _():
+            for k, zz, _, yy, tt in relations():
+                if k:
+                    spread_copy(g, k, zz, yy, tt).start()
+
+        @pl.when(end)
+        def _():
+            for k, zz, _, yy, tt in relations():
+                spread_copy(g, n_own + k, zz, yy, tt).start()
+
+    def slices(g, count):
+        ref = rs_bufs[g].at[pl.ds(0, count)]
+        return copy_to(ref, ref, rs_send.at[g], rs_recv.at[g], {"tx": mate})
+
+    def answers(g, count):
+        ref = rs_bufs[g].at[pl.ds(0, count)]
+        return copy_to(ref, ref, ag_send.at[g], ag_recv.at[g], {"tx": mate})
+
+    def settle(g):
+        @pl.when(inner)
+        def _():
+            slices(g, 2 * n_own - 1).wait_recv()
+            first, span = owner_rows(g, z, y, tx)
+            total = modes[g][pl.ds(pl.multiple_of(first, 8), span), :] + jnp.sum(rs_bufs[g][1:], axis=0)
+            sums[g][...] = total
+            dst = rows_of(ag_bufs[g], first, span)
+            for k, zz, ze, yy, tt in relations():
+                copy_to(sums[g], dst, ag_send.at[g], ag_recv.at[g], {"ty": 2 * ze + yy, "tx": tt}).start()
+                if k:
+                    copy_to(sums[g], dst, ag_send.at[g], ag_recv.at[g], {"ty": 2 * zz + yy, "tx": tt}).start()
+            ag_bufs[g][pl.ds(pl.multiple_of(first, 8), span), :] = total
+
+    def nudge_direct(g):
+        @pl.when(inner)
+        def _():
+            answers(g, n_own - 1).wait_recv()
+
+        @pl.when(end)
+        def _():
+            answers(g, n_own).wait_recv()
+        correct(g)
+
     last_chunk = {f: c for c, (f, _, _, _) in enumerate(chunks)}
     group_of = {f: g for g, fs in enumerate(groups) for f in fs}
     todo = {}
@@ -654,7 +740,8 @@
             project(g, f)
             if f == groups[g][-1]:
                 due = k
-                for step, gap in zip((scatter, reduce, hand_back, nudge), ADDS):
+                steps = (settle, nudge_direct) if g in direct else (scatter, reduce, hand_back, nudge)
+                for step, gap in zip(steps, ADDS[g]):
                     due += gap
                     todo.setdefault(due, []).append((step, g))
 
@@ -721,11 +808,21 @@
         for copy in want[1]:
             copy.wait_send()
     for g in range(n_groups):
-        swap_copy(g).wait_send()
-        back_copy(g).wait_send()
-        whole = rs_bufs[g]
-        copy_to(whole, whole, rs_send.at[g], rs_recv.at[g], {"tx": mate}).wait_send()
-        copy_to(whole, whole, ag_send.at[g], ag_recv.at[g], {"tx": mate}).wait_send()
+        if g in direct:
+            @pl.when(inner)
+            def _():
+                slices(g, n_own - 1).wait_send()
+                answers(g, 2 * n_own - 1).wait_send()
+
+            @pl.when(end)
+            def _():
+                slices(g, n_own).wait_send()
+        else:
+            swap_copy(g).wait_send()
+            back_copy(g).wait_send()
+            whole = rs_bufs[g]
+            copy_to(whole, whole, rs_send.at[g], rs_recv.at[g], {"tx": mate}).wait_send()
+            copy_to(whole, whole, ag_send.at[g], ag_recv.at[g], {"tx": mate}).wait_send()
 
 
 def ladder_call(
@@ -746,8 +843,10 @@
         + [pltpu.VMEM((2 * per_tile, c[2], BS), jnp.bfloat16) for c in chunks] * 2
         + [pltpu.VMEM((len(g) * 128, 128), jnp.float32) for g in groups]
         + [pltpu.VMEM((h, 128), jnp.float32) for h in halves] * 2
-        + [pltpu.VMEM((n_ty - 1, h // n_ty, 128), jnp.float32) for h in halves]
-        + [pltpu.VMEM((h // n_ty, 128), jnp.float32) for h in halves]
+        + [pltpu.VMEM((n_ty - 1, h // n_ty, 128), jnp.float32) for h in halves[:-1]]
+        + [pltpu.VMEM((n_ty * n_tx, 2 * halves[-1] // n_ty, 128), jnp.float32)]
+        + [pltpu.VMEM((h // n_ty, 128), jnp.float32) for h in halves[:-1]]
+        + [pltpu.VMEM((2 * halves[-1] // n_ty, 128), jnp.float32)]
         + [pltpu.VMEM((len(g) * 128, 128), jnp.float32) for g in groups]
         + [
             pltpu.VMEM((rows, 128), jnp.float32),

time: 79.5 us -> 74.3 us (0.935)
  Pallas kernels: 76.5 us -> 71.4 us
    pallas_call x1, Pallas kernels: 76.5 us -> 71.4 us  [ladder_call(): pl.pallas_call(functools.partial(ladder_kernel, n_ty, n_tx, chunks, group...]
where the time goes in v3:
time: 74.3 us; the launch traced here: 74.1 us
  Pallas kernels  71.4 us (96%)
  local copies, waits for them, and re-layouts  2.76 us (4%)
    pallas_call x1, Pallas kernels, ladder_call(): pl.pallas_call(functools.partial(ladder_kernel, n_ty, n_tx, chunks, group...  71.4 us
    unnamed x1, local copies, waits for them, and re-layouts  2.76 us

profile of v3, /device:TPU:1, one launch (start us, length us, event | category | flops | bytes accessed | tf_op | source)
XLA Modules:
  0.0 74.1 jit_solution(9199640769751458211)
XLA Ops:
  0.0 71.4 %remap_ladder.1 = f32[6,128,512]{2,1,0:T(8,128)} custom-call(bf16[6,128,512]{2,1,0:T(8,128)(2,1)} %fields.1, bf16[128,512]{1,0:T(8,128)(2,1)} %weights_hbm.1, s32[2,4]{1,0:T(2,128)} %bitcast.6, s32[2,4]{1,0:T(2,128)} %bitcast.7, bf16[6,6]{1,0:T(8,128)(2,1)} %coupling.1, f32[6,128,128]{2,1,0:T(8,128)} %driver_hbm.1, f32[6,128,128]{2,1,0:T(8,128)} %relaxation_hbm.1, ...), custom_call_target="tpu_custom_call" | custom-call | tf_op jit(solution)/shard_map/remap_ladder/pallas_call | solution.py:872
  71.4 2.8 %copy.11 = f32[6,128,512]{2,1,0:T(8,128)} copy(f32[6,128,512]{2,1,0:T(8,128)} %remap_ladder.1) | data formatting | bytes 3145728

commit v4 on v3

--- a/solution.py
+++ b/solution.py
@@ -13,7 +13,7 @@
 KMAX = 64
 GROUP = 2
 MESH = pl.DeviceIdType.MESH
-HI = lax.Precision.HIGHEST
+HI = lax.Precision.HIGH
 
 
 def wave_table(period):
@@ -288,7 +288,7 @@
 SPLIT = 2
 PATTERN = "PQPPQPPQPPQP"
 LAUNCH, SECOND, COLLECT, ANSWER, FINISH = 3, 1, 2, 3, 5
-ADDS = ((1, 2, 1, 1), (1, 3))
+ADDS = ((1, 2, 1, 1), (1, 2))
 GROUPS = (5, 1)
 
 
@@ -306,8 +306,9 @@
 def ladder_kernel(
     n_ty, n_tx, chunks, groups,
     fields, weights_hbm, tile_s, block_s, coupling, driver_hbm, relaxation_hbm, row_tab, row_tab_t, col_tab,
-    out, *scratch,
+    result, *scratch,
 ):
+    out, out_sem, *scratch = scratch
     n_fields, rows, cols = fields.shape
     n_chunks, n_groups = len(chunks), len(groups)
     gathered, asked, slots = (scratch[k * n_chunks : (k + 1) * n_chunks] for k in range(3))
@@ -667,6 +668,7 @@
                 span = slice(start, start + 2 * BS)
                 out[f, :, span] += lax.dot_general(
                     recon, col_b[span, :], (((1,), (1,)), ((), ())), precision=HI, preferred_element_type=jnp.float32)
+            pltpu.make_async_copy(out.at[f], result.at[f], out_sem.at[f]).start()
 
     n_own = n_ty * n_tx // 2
 
@@ -800,6 +802,8 @@
 
         if mode == "Q":
             to_mate(c, rail(c, tx)).wait_send()
+    for f in range(n_fields):
+        pltpu.make_async_copy(out.at[f], result.at[f], out_sem.at[f]).wait()
     for copy in want[0]:
         copy.wait_send()
 
@@ -839,7 +843,8 @@
     halves = [len(g) * 128 // n_tx for g in groups]
     asks = pltpu.SMEM((2, per_tile), jnp.int32)
     scratch = (
-        [pltpu.VMEM((n_ty * n_tx * per_tile, c[2], BS), jnp.bfloat16) for c in chunks]
+        [pltpu.VMEM((n_fields, rows, cols), jnp.float32), dma((n_fields,))]
+        + [pltpu.VMEM((n_ty * n_tx * per_tile, c[2], BS), jnp.bfloat16) for c in chunks]
         + [pltpu.VMEM((2 * per_tile, c[2], BS), jnp.bfloat16) for c in chunks] * 2
         + [pltpu.VMEM((len(g) * 128, 128), jnp.float32) for g in groups]
         + [pltpu.VMEM((h, 128), jnp.float32) for h in halves] * 2
@@ -873,7 +878,7 @@
         functools.partial(ladder_kernel, n_ty, n_tx, chunks, groups),
         out_shape=jax.ShapeDtypeStruct((n_fields, rows, cols), jnp.float32),
         in_specs=[hbm, hbm, smem, smem, vmem, hbm, hbm, hbm, hbm, hbm],
-        out_specs=vmem,
+        out_specs=hbm,
         scratch_shapes=scratch,
         compiler_params=pltpu.CompilerParams(
             collective_id=0, has_side_effects=True, vmem_limit_bytes=67043328

time: 74.3 us -> 73 us (0.983)
  Pallas kernels: 71.4 us -> 70.1 us
    pallas_call x1, Pallas kernels: 71.4 us -> 70.1 us  [ladder_call(): pl.pallas_call(functools.partial(ladder_kernel, n_ty, n_tx, chunks, group...]
where the time goes in v4:
time: 73 us; the launch traced here: 72.9 us
  Pallas kernels  70.1 us (96%)
  local copies, waits for them, and re-layouts  2.76 us (4%)
    pallas_call x1, Pallas kernels, ladder_call(): pl.pallas_call(functools.partial(ladder_kernel, n_ty, n_tx, chunks, group...  70.1 us
    unnamed x1, local copies, waits for them, and re-layouts  2.76 us

profile of v4, /device:TPU:1, one launch (start us, length us, event | category | flops | bytes accessed | tf_op | source)
XLA Modules:
  0.0 72.9 jit_solution(16755949225871696050)
XLA Ops:
  0.0 70.1 %remap_ladder.1 = f32[6,128,512]{2,1,0:T(8,128)} custom-call(bf16[6,128,512]{2,1,0:T(8,128)(2,1)} %fields.1, bf16[128,512]{1,0:T(8,128)(2,1)} %weights_hbm.1, s32[2,4]{1,0:T(2,128)} %bitcast.6, s32[2,4]{1,0:T(2,128)} %bitcast.7, bf16[6,6]{1,0:T(8,128)(2,1)} %coupling.1, f32[6,128,128]{2,1,0:T(8,128)} %driver_hbm.1, f32[6,128,128]{2,1,0:T(8,128)} %relaxation_hbm.1, ...), custom_call_target="tpu_custom_call" | custom-call | tf_op jit(solution)/shard_map/remap_ladder/pallas_call | solution.py:877
  70.1 2.8 %copy.11 = f32[6,128,512]{2,1,0:T(8,128)} copy(f32[6,128,512]{2,1,0:T(8,128)} %remap_ladder.1) | data formatting | bytes 3145728
